TPU v7x, 32 devices: a whole 2x2x4 slice. The times are simulated.
32 devices in a mesh: row: 4 (over y, core), col: 8 (over z, x).
Axes of the slice: x: 2, y: 2, z: 4, core: 2. Of those that a mesh axis runs over, the one named last changes fastest.
Arguments:
- obs_cell: int32 [32, 16, 32, 128], P(('row', 'col')), may hold values from 0 to 8388607, as said below
- obs_value: bfloat16 [32, 16, 32, 128], P(('row', 'col')), may hold values from -6 to 6
- obs_weight: bfloat16 [32, 16, 32, 128], P(('row', 'col')), may hold values from 0.5 to 2
- obs_count: int32 [32, 16, 32], P(('row', 'col')), may hold values from 0 to 128, as said below
- kappa_field: float32 [2048, 4096], P('row', 'col'), may hold values from 0.2 to 6
Outputs:
- solution_field: float32 [2048, 4096], P('row', 'col')
- residual: float32 [2048, 4096], P('row', 'col')
Inputs may be any that keep to these rules, and one draw needn't show every extreme that they name: `obs_cell`: block (s, t, d) holds observations for tile t of device d, where device d is number d // 8 along row and d % (8) along col, and tile t is number t // 4 among the device's tiles along rows and t % (4) along columns, each tile 128 by 128 cells; every slot of the block, padding included, names a cell of that tile as row * 4096 + column. Slots at positions obs_count and beyond are padding. For one owner device, chosen afresh in each draw, every block from every source and tile is full.
All inputs are finite; a program needn't handle non-finite values.
Results may differ from a plain program's by a relative error of at most 0.0029.
Values may be sent and summed in bfloat16 or wider, within the bound.
A program may use at most 64 MiB of HBM per device.

v0:
```python
from functools import partial
import jax
import jax.numpy as jnp
from jax import lax
from jax.sharding import PartitionSpec as P

TILE = 128
ITERS = 3
smooth_weight = 0.05


def extended(block, sides, width):
    for axis, dim in sides:
        count = lax.axis_size(axis)
        forward = [(i, i + 1) for i in range(count - 1)]
        backward = [(target, source) for source, target in forward]
        low = lax.ppermute(
            lax.slice_in_dim(block, block.shape[dim] - width, None, axis=dim), axis, forward
        )
        high = lax.ppermute(lax.slice_in_dim(block, 0, width, axis=dim), axis, backward)
        block = jnp.concatenate([low, block, high], axis=dim)
    return block


def stencil_step(padded, kappa_field):
    center = padded[1:-1, 1:-1]
    beside = padded[2:, 1:-1] + padded[:-2, 1:-1]
    beside = beside + padded[1:-1, 2:] + padded[1:-1, :-2]
    return (4.0 + kappa_field) * center - beside


def bin_tile(members, cols_all):
    cell_ids, obs_vals, obs_wts, is_live = members
    local_row = cell_ids // cols_all % TILE
    local_col = cell_ids % cols_all % TILE
    offsets = jnp.arange(TILE, dtype=jnp.int32)
    row_onehot = (local_row[:, None] == offsets[None, :]).astype(jnp.bfloat16)
    col_onehot = (local_col[:, None] == offsets[None, :]).astype(jnp.bfloat16)
    zero_fill = jnp.zeros_like(obs_wts)
    masked_weight = jnp.where(is_live, obs_wts, zero_fill)
    product = (obs_wts.astype(jnp.float32) * obs_vals.astype(jnp.float32)).astype(jnp.bfloat16)
    masked_resp = jnp.where(is_live, product, zero_fill)
    stacked = jnp.concatenate(
        [col_onehot * masked_weight[:, None], col_onehot * masked_resp[:, None]], axis=1
    )
    return lax.dot_general(
        row_onehot, stacked, (((0,), (0,)), ((), ())), preferred_element_type=jnp.float32
    )


def per_device(obs_cell, obs_value, obs_weight, obs_count, kappa_field):
    rows_dev, cols_dev = kappa_field.shape
    cols_all = cols_dev * lax.axis_size("col")
    tiles_dev = obs_cell.shape[1]
    block_rows = obs_cell.shape[3]
    got_cells, got_counts = (
        lax.all_to_all(obs_cell, ("row", "col"), split_axis=2, concat_axis=2, tiled=True),
        lax.all_to_all(obs_count, ("row", "col"), split_axis=2, concat_axis=2, tiled=True),
    )
    got_values, got_weights = (
        lax.all_to_all(obs_value, ("row", "col"), split_axis=2, concat_axis=2, tiled=True),
        lax.all_to_all(obs_weight, ("row", "col"), split_axis=2, concat_axis=2, tiled=True),
    )
    flat_rows = obs_cell.shape[2] * block_rows
    positions = jnp.arange(block_rows, dtype=jnp.int32)
    is_live = (positions[None, None, :] < got_counts.reshape(tiles_dev, -1)[:, :, None]).reshape(
        tiles_dev, flat_rows
    )
    members = (
        got_cells.reshape(tiles_dev, flat_rows),
        got_values.reshape(tiles_dev, flat_rows),
        got_weights.reshape(tiles_dev, flat_rows),
        is_live,
    )
    binned = lax.map(partial(bin_tile, cols_all=cols_all), members)
    tile_rows = rows_dev // TILE
    tile_cols = cols_dev // TILE
    binned = (
        binned.reshape(tile_rows, tile_cols, TILE, 2, TILE)
        .transpose(3, 0, 2, 1, 4)
        .reshape(2, rows_dev, cols_dev)
    )
    weight_field = binned[0]
    response = binned[1]

    def operate(field):
        first = extended(field, (("row", 0), ("col", 1)), 1)
        inner = stencil_step(first, kappa_field)
        second = extended(inner, (("row", 0), ("col", 1)), 1)
        return weight_field * field + smooth_weight * stencil_step(second, kappa_field)

    solution_field = jnp.zeros_like(response)
    residual = response

    def two_products(current, image):
        return lax.psum((jnp.sum(current * current), jnp.sum(current * image)), ("row", "col"))

    image = operate(residual)
    norm_now, curvature = two_products(residual, image)
    alpha = norm_now / curvature
    direction, along = (residual, image)
    for step in range(ITERS):
        solution_field = solution_field + alpha * direction
        residual = residual - alpha * along
        if step + 1 < ITERS:
            image = operate(residual)
            norm_next, curvature = two_products(residual, image)
            ratio = norm_next / norm_now
            alpha = norm_next / (curvature - ratio * norm_next / alpha)
            direction = residual + ratio * direction
            along = image + ratio * along
            norm_now = norm_next
    return (solution_field, residual)


def solution(mesh):
    placed = (
        P(("row", "col"), None, None, None),
        P(("row", "col"), None, None, None),
        P(("row", "col"), None, None, None),
        P(("row", "col"), None, None),
        P("row", "col"),
    )
    return jax.shard_map(
        per_device,
        mesh=mesh,
        in_specs=placed,
        out_specs=(P("row", "col"), P("row", "col")),
        check_vma=False,
    )
```

profile of v0, /device:TPU:0, one launch (start us, length us, event | category | flops | bytes accessed | tf_op | source)
XLA Modules:
  0.0 424.5 jit_solution(13311932666679719868)
XLA Ops:
  2.0 7.3 %all-to-all-start.1 = ((s32[1,16,32]{1,0,2:T(1,128)}), s32[1,16,32]{1,0,2:T(1,128)S(1)}, u32[]{:S(2)}, u32[]{:S(2)}) async-start(s32[1,16,32]{1,0,2:T(1,128)} %copy.16), calls=%async_computation.1 | async-start | bytes 32768 | tf_op jit(solution)/shard_map/all_to_all | solution.py:58
  11.0 5.5 %all-to-all-done.1 = s32[1,16,32]{1,0,2:T(1,128)S(1)} async-done(((s32[1,16,32]{1,0,2:T(1,128)}), s32[1,16,32]{1,0,2:T(1,128)S(1)}, u32[]{:S(2)}, u32[]{:S(2)}) %all-to-all-start.1) | async-done | bytes 2080 | tf_op jit(solution)/shard_map/all_to_all | solution.py:58
  16.4 2.6 all-to-all-start.3
  22.5 4.3 %all-to-all-done.3 = bf16[1,16,32,128]{3,1,0,2:T(8,128)(2,1)S(1)} async-done(((bf16[1,16,32,128]{3,1,0,2:T(8,128)(2,1)}), bf16[1,16,32,128]{3,1,0,2:T(8,128)(2,1)S(1)}, u32[]{:S(2)}, u32[]{:S(2)}) %all-to-all-start.3) | async-done | bytes 131104 | tf_op jit(solution)/shard_map/all_to_all | solution.py:61
  26.8 2.6 all-to-all-start.2
  30.3 6.8 %all-to-all-done.2 = bf16[1,16,32,128]{3,1,0,2:T(8,128)(2,1)S(1)} async-done(((bf16[1,16,32,128]{3,1,0,2:T(8,128)(2,1)}), bf16[1,16,32,128]{3,1,0,2:T(8,128)(2,1)S(1)}, u32[]{:S(2)}, u32[]{:S(2)}) %all-to-all-start.2) | async-done | bytes 131104 | tf_op jit(solution)/shard_map/all_to_all | solution.py:62
  37.2 2.6 all-to-all-start
  40.6 9.7 %all-to-all-done = s32[1,16,32,128]{3,1,0,2:T(8,128)S(1)} async-done(((s32[1,16,32,128]{3,1,0,2:T(8,128)}), s32[1,16,32,128]{3,1,0,2:T(8,128)S(1)}, u32[]{:S(2)}, u32[]{:S(2)}) %all-to-all-start) | async-done | bytes 262176 | tf_op jit(solution)/shard_map/all_to_all | solution.py:57
  50.5 83.1 %while.13 = (s32[]{:T(128)}, f32[16,128,256]{2,1,0:T(8,128)S(1)}, s32[16,4096]{1,0:T(8,128)S(1)}, pred[16,4096]{1,0:T(8,128)(4,1)}, bf16[16,4096]{1,0:T(8,128)(2,1)}, /*index=5*/bf16[16,4096]{1,0:T(8,128)(2,1)S(1)}, s32[]{:T(128)}) while((s32[]{:T(128)}, f32[16,128,256]{2,1,0:T(8,128)S(1)}, s32[16,4096]{1,0:T(8,128)S(1)}, ...), condition=%wide.region_1.2_spmd, body=%wide.region_0.1_spmd.sunk | while | flops 274919424 | bytes 4550757 | solution.py:75
  52.3 1.9 fusion.62
  57.5 1.9 fusion.62
  62.7 1.9 fusion.62
  67.9 1.9 fusion.62
  73.1 1.9 fusion.62
  88.7 1.9 fusion.62
  134.9 2.3 reshape.137
  139.8 2.1 collective-permute-start.1
  143.3 2.0 collective-permute-done
  146.7 4.6 %collective-permute-start.3 = (f32[514,1]{1,0:T(8,128)S(1)}, f32[514,1]{1,0:T(8,128)S(1)}, u32[]{:S(2)}, u32[]{:S(2)}) collective-permute-start(f32[514,1]{1,0:T(8,128)S(1)} %get-tuple-element.158), channel_id=1, source_target_pairs={{0,1},{1,2},{2,3},{3,4},{4,5},{5,6},{6,7},{8,9},{9,10},{10,11},{11... | collective-permute-start | bytes 6176 | tf_op jit(solution)/shard_map/ppermute | solution.py:17
  151.2 3.9 collective-permute-done.2
  155.2 6.6 %collective-permute-done.3 = f32[514,1]{1,0:T(8,128)S(1)} collective-permute-done((f32[514,1]{1,0:T(8,128)S(1)}, f32[514,1]{1,0:T(8,128)S(1)}, u32[]{:S(2)}, u32[]{:S(2)}) %collective-permute-start.3) | collective-permute-done | bytes 2088 | tf_op jit(solution)/shard_map/ppermute | solution.py:17
  162.5 2.2 collective-permute-start.5
  169.3 4.8 %collective-permute-start.7 = (f32[514,1]{1,0:T(8,128)S(1)}, f32[514,1]{1,0:T(8,128)S(1)}, u32[]{:S(2)}, u32[]{:S(2)}) collective-permute-start(f32[514,1]{1,0:T(8,128)S(1)} %get-tuple-element.156), channel_id=1, source_target_pairs={{0,1},{1,2},{2,3},{3,4},{4,5},{5,6},{6,7},{8,9},{9,10},{10,11},{11... | collective-permute-start | bytes 6176 | tf_op jit(solution)/shard_map/ppermute | solution.py:17
  174.1 4.1 collective-permute-done.6
  178.2 7.2 %collective-permute-done.7 = f32[514,1]{1,0:T(8,128)S(1)} collective-permute-done((f32[514,1]{1,0:T(8,128)S(1)}, f32[514,1]{1,0:T(8,128)S(1)}, u32[]{:S(2)}, u32[]{:S(2)}) %collective-permute-start.7) | collective-permute-done | bytes 2088 | tf_op jit(solution)/shard_map/ppermute | solution.py:17
  185.4 2.6 multiply_reduce_fusion.4
  188.0 39.1 %all-reduce.2 = (f32[]{:T(128)}, f32[]{:T(128)}) all-reduce(f32[]{:T(128)} %get-tuple-element.144, f32[]{:T(128)} %get-tuple-element.134), channel_id=1, replica_groups=mesh['row'=4,'col'=8] {'row','col'}, use_global_device_ids=true, to_apply=%region_3.4 | all-reduce | flops 2 | bytes 16 | tf_op jit(solution)/shard_map/psum | solution.py:96
  232.4 4.5 %collective-permute-done.8 = f32[1,512]{1,0:T(1,128)S(1)} collective-permute-done((f32[1,512]{1,0:T(1,128)S(1)}, f32[1,512]{1,0:T(1,128)S(1)}, u32[]{:S(2)}, u32[]{:S(2)}) %collective-permute-start.8) | collective-permute-done | bytes 2080 | tf_op jit(solution)/shard_map/ppermute | solution.py:20
  238.4 4.7 %collective-permute-start.11 = (f32[514,1]{1,0:T(8,128)S(1)}, f32[514,1]{1,0:T(8,128)S(1)}, u32[]{:S(2)}, u32[]{:S(2)}) collective-permute-start(f32[514,1]{1,0:T(8,128)S(1)} %get-tuple-element.154), channel_id=1, source_target_pairs={{0,1},{1,2},{2,3},{3,4},{4,5},{5,6},{6,7},{8,9},{9,10},{10,11},{11... | collective-permute-start | bytes 6176 | tf_op jit(solution)/shard_map/ppermute | solution.py:17
  243.1 3.7 collective-permute-done.10
  246.8 7.3 %collective-permute-done.11 = f32[514,1]{1,0:T(8,128)S(1)} collective-permute-done((f32[514,1]{1,0:T(8,128)S(1)}, f32[514,1]{1,0:T(8,128)S(1)}, u32[]{:S(2)}, u32[]{:S(2)}) %collective-permute-start.11) | collective-permute-done | bytes 2088 | tf_op jit(solution)/shard_map/ppermute | solution.py:17
  254.9 2.2 collective-permute-start.13
  261.6 5.0 %collective-permute-start.15 = (f32[514,1]{1,0:T(8,128)S(1)}, f32[514,1]{1,0:T(8,128)S(1)}, u32[]{:S(2)}, u32[]{:S(2)}) collective-permute-start(f32[514,1]{1,0:T(8,128)S(1)} %get-tuple-element.152), channel_id=1, source_target_pairs={{0,1},{1,2},{2,3},{3,4},{4,5},{5,6},{6,7},{8,9},{9,10},{10,11},{11... | collective-permute-start | bytes 6176 | tf_op jit(solution)/shard_map/ppermute | solution.py:17
  266.6 3.9 collective-permute-done.14
  270.6 7.2 %collective-permute-done.15 = f32[514,1]{1,0:T(8,128)S(1)} collective-permute-done((f32[514,1]{1,0:T(8,128)S(1)}, f32[514,1]{1,0:T(8,128)S(1)}, u32[]{:S(2)}, u32[]{:S(2)}) %collective-permute-start.15) | collective-permute-done | bytes 2088 | tf_op jit(solution)/shard_map/ppermute | solution.py:17
  277.8 2.6 multiply_reduce_fusion.2
  280.4 40.2 %all-reduce.1 = (f32[]{:T(128)}, f32[]{:T(128)}) all-reduce(f32[]{:T(128)} %get-tuple-element.113, f32[]{:T(128)} %get-tuple-element.112), channel_id=1, replica_groups=mesh['row'=4,'col'=8] {'row','col'}, use_global_device_ids=true, to_apply=%region_7.8 | all-reduce | flops 2 | bytes 16 | tf_op jit(solution)/shard_map/psum | solution.py:96
  329.5 4.5 %collective-permute-done.16 = f32[1,512]{1,0:T(1,128)S(1)} collective-permute-done((f32[1,512]{1,0:T(1,128)S(1)}, f32[1,512]{1,0:T(1,128)S(1)}, u32[]{:S(2)}, u32[]{:S(2)}) %collective-permute-start.16) | collective-permute-done | bytes 2080 | tf_op jit(solution)/shard_map/ppermute | solution.py:20
  335.5 4.7 %collective-permute-start.19 = (f32[514,1]{1,0:T(8,128)S(1)}, f32[514,1]{1,0:T(8,128)S(1)}, u32[]{:S(2)}, u32[]{:S(2)}) collective-permute-start(f32[514,1]{1,0:T(8,128)S(1)} %get-tuple-element.150), channel_id=1, source_target_pairs={{0,1},{1,2},{2,3},{3,4},{4,5},{5,6},{6,7},{8,9},{9,10},{10,11},{11... | collective-permute-start | bytes 6176 | tf_op jit(solution)/shard_map/ppermute | solution.py:17
  340.2 3.7 collective-permute-done.18
  343.9 7.3 %collective-permute-done.19 = f32[514,1]{1,0:T(8,128)S(1)} collective-permute-done((f32[514,1]{1,0:T(8,128)S(1)}, f32[514,1]{1,0:T(8,128)S(1)}, u32[]{:S(2)}, u32[]{:S(2)}) %collective-permute-start.19) | collective-permute-done | bytes 2088 | tf_op jit(solution)/shard_map/ppermute | solution.py:17
  352.0 2.2 collective-permute-start.21
  358.7 4.8 %collective-permute-start.23 = (f32[514,1]{1,0:T(8,128)S(1)}, f32[514,1]{1,0:T(8,128)S(1)}, u32[]{:S(2)}, u32[]{:S(2)}) collective-permute-start(f32[514,1]{1,0:T(8,128)S(1)} %get-tuple-element.148), channel_id=1, source_target_pairs={{0,1},{1,2},{2,3},{3,4},{4,5},{5,6},{6,7},{8,9},{9,10},{10,11},{11... | collective-permute-start | bytes 6176 | tf_op jit(solution)/shard_map/ppermute | solution.py:17
  363.5 4.1 collective-permute-done.22
  367.6 7.2 %collective-permute-done.23 = f32[514,1]{1,0:T(8,128)S(1)} collective-permute-done((f32[514,1]{1,0:T(8,128)S(1)}, f32[514,1]{1,0:T(8,128)S(1)}, u32[]{:S(2)}, u32[]{:S(2)}) %collective-permute-start.23) | collective-permute-done | bytes 2088 | tf_op jit(solution)/shard_map/ppermute | solution.py:17
  374.9 2.6 multiply_reduce_fusion
  377.5 39.0 %all-reduce = (f32[]{:T(128)}, f32[]{:T(128)}) all-reduce(f32[]{:T(128)} %get-tuple-element.111, f32[]{:T(128)} %get-tuple-element.110), channel_id=1, replica_groups=mesh['row'=4,'col'=8] {'row','col'}, use_global_device_ids=true, to_apply=%region_11.12 | all-reduce | flops 2 | bytes 16 | tf_op jit(solution)/shard_map/psum | solution.py:96
  420.3 4.3 %multiply_subtract_fusion = (f32[512,512]{1,0:T(8,128)}, f32[512,512]{1,0:T(8,128)}) fusion(f32[512,512]{1,0:T(8,128)S(1)} %multiply_subtract_fusion.1, f32[512,512]{1,0:T(8,128)} %get-tuple-element.132, f32[]{:T(128)S(6)} %div.37, f32[]{:T(128)S(6)} %div.39, f32[512,512]{1,0:T(8,128)} %get-tuple-element.133, f32[512,512]{1,0:T(8,128)} %get-tuple-element.135, ...), kind=kLoop, calls=%fused_computation.118 | loop fusion | flops 3932160 | bytes 8388628 | tf_op jit(solution)/shard_map/sub | solution.py:104
  (175 shorter events, 112.9 us)
Async XLA Ops:
  2.0 14.4 %all-to-all-start.1 = ((s32[1,16,32]{1,0,2:T(1,128)}), s32[1,16,32]{1,0,2:T(1,128)S(1)}, u32[]{:S(2)}, u32[]{:S(2)}) async-start(s32[1,16,32]{1,0,2:T(1,128)} %copy.16), calls=%async_computation.1 | async-start | bytes 32768 | tf_op jit(solution)/shard_map/all_to_all | solution.py:58
  16.4 10.4 %all-to-all-start.3 = ((bf16[1,16,32,128]{3,1,0,2:T(8,128)(2,1)}), bf16[1,16,32,128]{3,1,0,2:T(8,128)(2,1)S(1)}, u32[]{:S(2)}, u32[]{:S(2)}) async-start(bf16[1,16,32,128]{3,1,0,2:T(8,128)(2,1)} %copy.20), calls=%async_computation.3 | async-start | bytes 262144 | tf_op jit(solution)/shard_map/all_to_all | solution.py:61
  26.8 10.4 %all-to-all-start.2 = ((bf16[1,16,32,128]{3,1,0,2:T(8,128)(2,1)}), bf16[1,16,32,128]{3,1,0,2:T(8,128)(2,1)S(1)}, u32[]{:S(2)}, u32[]{:S(2)}) async-start(bf16[1,16,32,128]{3,1,0,2:T(8,128)(2,1)} %copy.18), calls=%async_computation.2 | async-start | bytes 262144 | tf_op jit(solution)/shard_map/all_to_all | solution.py:62
  37.2 13.0 %all-to-all-start = ((s32[1,16,32,128]{3,1,0,2:T(8,128)}), s32[1,16,32,128]{3,1,0,2:T(8,128)S(1)}, u32[]{:S(2)}, u32[]{:S(2)}) async-start(s32[1,16,32,128]{3,1,0,2:T(8,128)} %copy.14), calls=%async_computation | async-start | bytes 524288 | tf_op jit(solution)/shard_map/all_to_all | solution.py:57
  133.6 1.3 copy-start.5
  139.7 45.7 %copy-start.2 = (f32[1,4,128,4,128]{4,3,2,1,0:T(4,128)}, f32[1,4,128,4,128]{4,3,2,1,0:T(4,128)S(1)}, u32[]{:S(2)}) copy-start(f32[1,4,128,4,128]{4,3,2,1,0:T(4,128)S(1)} %get-tuple-element.145) | copy-start | bytes 3145732
  139.8 88.6 %copy-start.1 = (f32[1,4,128,4,128]{4,3,2,1,0:T(4,128)}, f32[1,4,128,4,128]{4,3,2,1,0:T(4,128)S(1)}, u32[]{:S(2)}) copy-start(f32[1,4,128,4,128]{4,3,2,1,0:T(4,128)S(1)} %get-tuple-element.146) | copy-start | bytes 3145732
  139.8 22.0 %copy-start = (f32[512,512]{1,0:T(8,128)S(1)}, f32[512,512]{1,0:T(8,128)}, u32[]{:S(2)}) copy-start(f32[512,512]{1,0:T(8,128)} %param.11) | copy-start | bytes 3145732
  139.8 3.4 collective-permute-start.1
  141.9 3.3 collective-permute-start
  145.4 9.8 %collective-permute-start.2 = (f32[514,1]{1,0:T(8,128)S(1)}, f32[514,1]{1,0:T(8,128)S(1)}, u32[]{:S(2)}, u32[]{:S(2)}) collective-permute-start(f32[514,1]{1,0:T(8,128)S(1)} %get-tuple-element.157), channel_id=1, source_target_pairs={{1,0},{2,1},{3,2},{4,3},{5,4},{6,5},{7,6},{9,8},{10,9},{11,10},{12... | collective-permute-start | bytes 6176 | tf_op jit(solution)/shard_map/ppermute | solution.py:20
  146.7 15.1 %collective-permute-start.3 = (f32[514,1]{1,0:T(8,128)S(1)}, f32[514,1]{1,0:T(8,128)S(1)}, u32[]{:S(2)}, u32[]{:S(2)}) collective-permute-start(f32[514,1]{1,0:T(8,128)S(1)} %get-tuple-element.158), channel_id=1, source_target_pairs={{0,1},{1,2},{2,3},{3,4},{4,5},{5,6},{6,7},{8,9},{9,10},{10,11},{11... | collective-permute-start | bytes 6176 | tf_op jit(solution)/shard_map/ppermute | solution.py:17
  162.5 3.5 collective-permute-start.5
  164.7 3.1 collective-permute-start.4
  168.0 10.3 %collective-permute-start.6 = (f32[514,1]{1,0:T(8,128)S(1)}, f32[514,1]{1,0:T(8,128)S(1)}, u32[]{:S(2)}, u32[]{:S(2)}) collective-permute-start(f32[514,1]{1,0:T(8,128)S(1)} %get-tuple-element.155), channel_id=1, source_target_pairs={{1,0},{2,1},{3,2},{4,3},{5,4},{6,5},{7,6},{9,8},{10,9},{11,10},{12... | collective-permute-start | bytes 6176 | tf_op jit(solution)/shard_map/ppermute | solution.py:20
  169.3 16.2 %collective-permute-start.7 = (f32[514,1]{1,0:T(8,128)S(1)}, f32[514,1]{1,0:T(8,128)S(1)}, u32[]{:S(2)}, u32[]{:S(2)}) collective-permute-start(f32[514,1]{1,0:T(8,128)S(1)} %get-tuple-element.156), channel_id=1, source_target_pairs={{0,1},{1,2},{2,3},{3,4},{4,5},{5,6},{6,7},{8,9},{9,10},{10,11},{11... | collective-permute-start | bytes 6176 | tf_op jit(solution)/shard_map/ppermute | solution.py:17
  229.8 2.6 collective-permute-start.9
  231.1 5.8 %collective-permute-start.8 = (f32[1,512]{1,0:T(1,128)S(1)}, f32[1,512]{1,0:T(1,128)S(1)}, u32[]{:S(2)}, u32[]{:S(2)}) collective-permute-start(f32[1,512]{1,0:T(1,128)S(1)} %get-tuple-element.168), channel_id=1, source_target_pairs={{8,0},{16,8},{24,16},{9,1},{17,9},{25,17},{10,2},{18,10},{26,18},{... | collective-permute-start | bytes 6152 | tf_op jit(solution)/shard_map/ppermute | solution.py:20
  237.1 9.7 %collective-permute-start.10 = (f32[514,1]{1,0:T(8,128)S(1)}, f32[514,1]{1,0:T(8,128)S(1)}, u32[]{:S(2)}, u32[]{:S(2)}) collective-permute-start(f32[514,1]{1,0:T(8,128)S(1)} %get-tuple-element.153), channel_id=1, source_target_pairs={{1,0},{2,1},{3,2},{4,3},{5,4},{6,5},{7,6},{9,8},{10,9},{11,10},{12... | collective-permute-start | bytes 6176 | tf_op jit(solution)/shard_map/ppermute | solution.py:20
  238.4 39.4 %copy-start.3 = (f32[1,4,128,4,128]{4,3,2,1,0:T(4,128)S(1)}, f32[1,4,128,4,128]{4,3,2,1,0:T(4,128)}, u32[]{:S(2)}) copy-start(f32[1,4,128,4,128]{4,3,2,1,0:T(4,128)} %copy-done.2) | copy-start | bytes 3145732
  238.4 15.7 %collective-permute-start.11 = (f32[514,1]{1,0:T(8,128)S(1)}, f32[514,1]{1,0:T(8,128)S(1)}, u32[]{:S(2)}, u32[]{:S(2)}) collective-permute-start(f32[514,1]{1,0:T(8,128)S(1)} %get-tuple-element.154), channel_id=1, source_target_pairs={{0,1},{1,2},{2,3},{3,4},{4,5},{5,6},{6,7},{8,9},{9,10},{10,11},{11... | collective-permute-start | bytes 6176 | tf_op jit(solution)/shard_map/ppermute | solution.py:17
  254.9 3.5 collective-permute-start.13
  257.1 3.1 collective-permute-start.12
  260.3 10.3 %collective-permute-start.14 = (f32[514,1]{1,0:T(8,128)S(1)}, f32[514,1]{1,0:T(8,128)S(1)}, u32[]{:S(2)}, u32[]{:S(2)}) collective-permute-start(f32[514,1]{1,0:T(8,128)S(1)} %get-tuple-element.151), channel_id=1, source_target_pairs={{1,0},{2,1},{3,2},{4,3},{5,4},{6,5},{7,6},{9,8},{10,9},{11,10},{12... | collective-permute-start | bytes 6176 | tf_op jit(solution)/shard_map/ppermute | solution.py:20
  261.6 16.2 %collective-permute-start.15 = (f32[514,1]{1,0:T(8,128)S(1)}, f32[514,1]{1,0:T(8,128)S(1)}, u32[]{:S(2)}, u32[]{:S(2)}) collective-permute-start(f32[514,1]{1,0:T(8,128)S(1)} %get-tuple-element.152), channel_id=1, source_target_pairs={{0,1},{1,2},{2,3},{3,4},{4,5},{5,6},{6,7},{8,9},{9,10},{10,11},{11... | collective-permute-start | bytes 6176 | tf_op jit(solution)/shard_map/ppermute | solution.py:17
  326.9 2.6 collective-permute-start.17
  328.2 5.8 %collective-permute-start.16 = (f32[1,512]{1,0:T(1,128)S(1)}, f32[1,512]{1,0:T(1,128)S(1)}, u32[]{:S(2)}, u32[]{:S(2)}) collective-permute-start(f32[1,512]{1,0:T(1,128)S(1)} %get-tuple-element.164), channel_id=1, source_target_pairs={{8,0},{16,8},{24,16},{9,1},{17,9},{25,17},{10,2},{18,10},{26,18},{... | collective-permute-start | bytes 6152 | tf_op jit(solution)/shard_map/ppermute | solution.py:20
  334.2 9.7 %collective-permute-start.18 = (f32[514,1]{1,0:T(8,128)S(1)}, f32[514,1]{1,0:T(8,128)S(1)}, u32[]{:S(2)}, u32[]{:S(2)}) collective-permute-start(f32[514,1]{1,0:T(8,128)S(1)} %get-tuple-element.149), channel_id=1, source_target_pairs={{1,0},{2,1},{3,2},{4,3},{5,4},{6,5},{7,6},{9,8},{10,9},{11,10},{12... | collective-permute-start | bytes 6176 | tf_op jit(solution)/shard_map/ppermute | solution.py:20
  335.5 39.4 %copy-start.4 = (f32[1,4,128,4,128]{4,3,2,1,0:T(4,128)S(1)}, f32[1,4,128,4,128]{4,3,2,1,0:T(4,128)}, u32[]{:S(2)}) copy-start(f32[1,4,128,4,128]{4,3,2,1,0:T(4,128)} %copy-done.2) | copy-start | bytes 3145732
  335.5 15.7 %collective-permute-start.19 = (f32[514,1]{1,0:T(8,128)S(1)}, f32[514,1]{1,0:T(8,128)S(1)}, u32[]{:S(2)}, u32[]{:S(2)}) collective-permute-start(f32[514,1]{1,0:T(8,128)S(1)} %get-tuple-element.150), channel_id=1, source_target_pairs={{0,1},{1,2},{2,3},{3,4},{4,5},{5,6},{6,7},{8,9},{9,10},{10,11},{11... | collective-permute-start | bytes 6176 | tf_op jit(solution)/shard_map/ppermute | solution.py:17
  352.0 3.5 collective-permute-start.21
  354.2 3.1 collective-permute-start.20
  357.4 10.3 %collective-permute-start.22 = (f32[514,1]{1,0:T(8,128)S(1)}, f32[514,1]{1,0:T(8,128)S(1)}, u32[]{:S(2)}, u32[]{:S(2)}) collective-permute-start(f32[514,1]{1,0:T(8,128)S(1)} %get-tuple-element.147), channel_id=1, source_target_pairs={{1,0},{2,1},{3,2},{4,3},{5,4},{6,5},{7,6},{9,8},{10,9},{11,10},{12... | collective-permute-start | bytes 6176 | tf_op jit(solution)/shard_map/ppermute | solution.py:20
  358.7 16.2 %collective-permute-start.23 = (f32[514,1]{1,0:T(8,128)S(1)}, f32[514,1]{1,0:T(8,128)S(1)}, u32[]{:S(2)}, u32[]{:S(2)}) collective-permute-start(f32[514,1]{1,0:T(8,128)S(1)} %get-tuple-element.148), channel_id=1, source_target_pairs={{0,1},{1,2},{2,3},{3,4},{4,5},{5,6},{6,7},{8,9},{9,10},{10,11},{11... | collective-permute-start | bytes 6176 | tf_op jit(solution)/shard_map/ppermute | solution.py:17
where the time goes:
time: 428 us; the launch traced here: 425 us
  blocking collectives  118 us (28%)
  waiting for transfers between devices  109 us (25%)
  starting transfers between devices  70.5 us (16%)
  other arithmetic  66.7 us (16%)
  local copies, waits for them, and re-layouts  26.2 us (6%)
  matrix products  22.6 us (5%)
  between operations  10.6 us (2%)
    psum x3, blocking collectives, two_products(): lax.psum((jnp.sum(current * current), jnp.sum(current * image)), ('row',...  118 us
    ppermute x12, waiting for transfers between devices, extended(): lax.ppermute(lax.slice_in_dim(block, block.shape[dim] - width, None, axis...  43 us
    ppermute x12, starting transfers between devices, extended(): lax.ppermute(lax.slice_in_dim(block, block.shape[dim] - width, None, axis...  40 us
    ppermute x12, waiting for transfers between devices, extended(): lax.ppermute(lax.slice_in_dim(block, 0, width, axis=dim), axis, backward)  39.6 us
    mul x16, other arithmetic, bin_tile(): col_onehot * masked_weight[:, None]  30.8 us
    dot_general x16, matrix products, bin_tile(): lax.dot_general(row_onehot, stacked, (((0,), (0,)), ((), ())), preferred_...  22.6 us
    ppermute x12, starting transfers between devices, extended(): lax.ppermute(lax.slice_in_dim(block, 0, width, axis=dim), axis, backward)  15.5 us
    convert_element_type x16, other arithmetic, bin_tile(): obs_vals.astype(jnp.float32)  14.7 us
  transfers between devices with their start and end apart: 28, of which 22 were waited for; matrix products, arithmetic and copies ran while one was open for 2% of the time, Pallas kernels for 0%

commit v1 on v0

--- a/solution.py
+++ b/solution.py
@@ -93,7 +93,9 @@
     residual = response
 
     def two_products(current, image):
-        return lax.psum((jnp.sum(current * current), jnp.sum(current * image)), ("row", "col"))
+        return lax.psum(
+            lax.psum((jnp.sum(current * current), jnp.sum(current * image)), "col"), "row"
+        )
 
     image = operate(residual)
     norm_now, curvature = two_products(residual, image)

time: 428 us -> 380 us (0.89)
  blocking collectives: 118 us -> 80 us
  waiting for transfers between devices: 109 us -> 98.8 us
    psum x3 -> x6, blocking collectives: 118 us -> 80 us  [the longest x3 60.8 us: two_products(): lax.psum((jnp.sum(current * current), jnp.sum(current * image)), 'col')]
    ppermute x12, waiting for transfers between devices: 43 us -> 37.6 us  [extended(): lax.ppermute(lax.slice_in_dim(block, block.shape[dim] - width, None, axis...]
    ppermute x12, waiting for transfers between devices: 39.6 us -> 35 us  [extended(): lax.ppermute(lax.slice_in_dim(block, 0, width, axis=dim), axis, backward)]
where the time goes in v1:
time: 380 us; the launch traced here: 377 us
  waiting for transfers between devices  98.8 us (26%)
  blocking collectives  80 us (21%)
  starting transfers between devices  71.3 us (19%)
  other arithmetic  66.6 us (18%)
  local copies, waits for them, and re-layouts  26.2 us (7%)
  matrix products  22.6 us (6%)
  between operations  10.8 us (3%)
    psum x3, blocking collectives, two_products(): lax.psum((jnp.sum(current * current), jnp.sum(current * image)), 'col')  60.8 us
    ppermute x12, starting transfers between devices, extended(): lax.ppermute(lax.slice_in_dim(block, block.shape[dim] - width, None, axis...  40.7 us
    ppermute x12, waiting for transfers between devices, extended(): lax.ppermute(lax.slice_in_dim(block, block.shape[dim] - width, None, axis...  37.6 us
    ppermute x12, waiting for transfers between devices, extended(): lax.ppermute(lax.slice_in_dim(block, 0, width, axis=dim), axis, backward)  35 us
    mul x16, other arithmetic, bin_tile(): col_onehot * masked_weight[:, None]  30.8 us
    dot_general x16, matrix products, bin_tile(): lax.dot_general(row_onehot, stacked, (((0,), (0,)), ((), ())), preferred_...  22.6 us
    psum x3, blocking collectives, two_products(): lax.psum(lax.psum((jnp.sum(current * current), jnp.sum(current * image)),...  19.2 us
    ppermute x12, starting transfers between devices, extended(): lax.ppermute(lax.slice_in_dim(block, 0, width, axis=dim), axis, backward)  15.5 us
  transfers between devices with their start and end apart: 28, of which 22 were waited for; matrix products, arithmetic and copies ran while one was open for 2% of the time, Pallas kernels for 0%

profile of v1, /device:TPU:0, one launch (start us, length us, event | category | flops | bytes accessed | tf_op | source)
XLA Modules:
  0.0 377.1 jit_solution(11699979559293590564)
XLA Ops:
  2.0 7.3 %all-to-all-start.1 = ((s32[1,16,32]{1,0,2:T(1,128)}), s32[1,16,32]{1,0,2:T(1,128)S(1)}, u32[]{:S(2)}, u32[]{:S(2)}) async-start(s32[1,16,32]{1,0,2:T(1,128)} %copy.16), calls=%async_computation.1 | async-start | bytes 32768 | tf_op jit(solution)/shard_map/all_to_all | solution.py:58
  11.0 5.5 %all-to-all-done.1 = s32[1,16,32]{1,0,2:T(1,128)S(1)} async-done(((s32[1,16,32]{1,0,2:T(1,128)}), s32[1,16,32]{1,0,2:T(1,128)S(1)}, u32[]{:S(2)}, u32[]{:S(2)}) %all-to-all-start.1) | async-done | bytes 2080 | tf_op jit(solution)/shard_map/all_to_all | solution.py:58
  16.4 2.6 all-to-all-start.3
  22.5 4.3 %all-to-all-done.3 = bf16[1,16,32,128]{3,1,0,2:T(8,128)(2,1)S(1)} async-done(((bf16[1,16,32,128]{3,1,0,2:T(8,128)(2,1)}), bf16[1,16,32,128]{3,1,0,2:T(8,128)(2,1)S(1)}, u32[]{:S(2)}, u32[]{:S(2)}) %all-to-all-start.3) | async-done | bytes 131104 | tf_op jit(solution)/shard_map/all_to_all | solution.py:61
  26.8 2.6 all-to-all-start.2
  30.3 6.8 %all-to-all-done.2 = bf16[1,16,32,128]{3,1,0,2:T(8,128)(2,1)S(1)} async-done(((bf16[1,16,32,128]{3,1,0,2:T(8,128)(2,1)}), bf16[1,16,32,128]{3,1,0,2:T(8,128)(2,1)S(1)}, u32[]{:S(2)}, u32[]{:S(2)}) %all-to-all-start.2) | async-done | bytes 131104 | tf_op jit(solution)/shard_map/all_to_all | solution.py:62
  37.2 2.6 all-to-all-start
  40.6 9.7 %all-to-all-done = s32[1,16,32,128]{3,1,0,2:T(8,128)S(1)} async-done(((s32[1,16,32,128]{3,1,0,2:T(8,128)}), s32[1,16,32,128]{3,1,0,2:T(8,128)S(1)}, u32[]{:S(2)}, u32[]{:S(2)}) %all-to-all-start) | async-done | bytes 262176 | tf_op jit(solution)/shard_map/all_to_all | solution.py:57
  50.5 83.1 %while.13 = (s32[]{:T(128)}, f32[16,128,256]{2,1,0:T(8,128)S(1)}, s32[16,4096]{1,0:T(8,128)S(1)}, pred[16,4096]{1,0:T(8,128)(4,1)}, bf16[16,4096]{1,0:T(8,128)(2,1)}, /*index=5*/bf16[16,4096]{1,0:T(8,128)(2,1)S(1)}, s32[]{:T(128)}) while((s32[]{:T(128)}, f32[16,128,256]{2,1,0:T(8,128)S(1)}, s32[16,4096]{1,0:T(8,128)S(1)}, ...), condition=%wide.region_1.2_spmd, body=%wide.region_0.1_spmd.sunk | while | flops 274919424 | bytes 4550757 | solution.py:75
  52.3 1.9 fusion.62
  57.5 1.9 fusion.62
  62.7 1.9 fusion.62
  73.1 1.9 fusion.62
  88.7 1.9 fusion.62
  134.9 2.3 reshape.137
  139.9 2.1 collective-permute-start.1
  143.3 2.0 collective-permute-done
  146.7 4.6 %collective-permute-start.3 = (f32[514,1]{1,0:T(8,128)S(1)}, f32[514,1]{1,0:T(8,128)S(1)}, u32[]{:S(2)}, u32[]{:S(2)}) collective-permute-start(f32[514,1]{1,0:T(8,128)S(1)} %get-tuple-element.164), channel_id=1, source_target_pairs={{0,1},{1,2},{2,3},{3,4},{4,5},{5,6},{6,7},{8,9},{9,10},{10,11},{11... | collective-permute-start | bytes 6176 | tf_op jit(solution)/shard_map/ppermute | solution.py:17
  151.3 3.9 %collective-permute-done.2 = f32[514,1]{1,0:T(8,128)S(1)} collective-permute-done((f32[514,1]{1,0:T(8,128)S(1)}, f32[514,1]{1,0:T(8,128)S(1)}, u32[]{:S(2)}, u32[]{:S(2)}) %collective-permute-start.2) | collective-permute-done | bytes 2088 | tf_op jit(solution)/shard_map/ppermute | solution.py:20
  155.2 6.6 %collective-permute-done.3 = f32[514,1]{1,0:T(8,128)S(1)} collective-permute-done((f32[514,1]{1,0:T(8,128)S(1)}, f32[514,1]{1,0:T(8,128)S(1)}, u32[]{:S(2)}, u32[]{:S(2)}) %collective-permute-start.3) | collective-permute-done | bytes 2088 | tf_op jit(solution)/shard_map/ppermute | solution.py:17
  162.5 2.2 collective-permute-start.5
  169.3 4.8 %collective-permute-start.7 = (f32[514,1]{1,0:T(8,128)S(1)}, f32[514,1]{1,0:T(8,128)S(1)}, u32[]{:S(2)}, u32[]{:S(2)}) collective-permute-start(f32[514,1]{1,0:T(8,128)S(1)} %get-tuple-element.162), channel_id=1, source_target_pairs={{0,1},{1,2},{2,3},{3,4},{4,5},{5,6},{6,7},{8,9},{9,10},{10,11},{11... | collective-permute-start | bytes 6176 | tf_op jit(solution)/shard_map/ppermute | solution.py:17
  174.1 4.1 %collective-permute-done.6 = f32[514,1]{1,0:T(8,128)S(1)} collective-permute-done((f32[514,1]{1,0:T(8,128)S(1)}, f32[514,1]{1,0:T(8,128)S(1)}, u32[]{:S(2)}, u32[]{:S(2)}) %collective-permute-start.6) | collective-permute-done | bytes 2088 | tf_op jit(solution)/shard_map/ppermute | solution.py:20
  178.2 7.2 %collective-permute-done.7 = f32[514,1]{1,0:T(8,128)S(1)} collective-permute-done((f32[514,1]{1,0:T(8,128)S(1)}, f32[514,1]{1,0:T(8,128)S(1)}, u32[]{:S(2)}, u32[]{:S(2)}) %collective-permute-start.7) | collective-permute-done | bytes 2088 | tf_op jit(solution)/shard_map/ppermute | solution.py:17
  185.5 2.6 multiply_reduce_fusion.4
  188.0 20.3 %all-reduce.2 = (f32[]{:T(128)}, f32[]{:T(128)}) all-reduce(f32[]{:T(128)} %get-tuple-element.150, f32[]{:T(128)} %get-tuple-element.140), channel_id=1, replica_groups=mesh['row'=4,'col'=8] {'col'}, use_global_device_ids=true, to_apply=%region_3.4 | all-reduce | flops 2 | bytes 16 | tf_op jit(solution)/shard_map/psum | solution.py:97
  208.3 6.4 %all-reduce.5 = (f32[]{:T(128)}, f32[]{:T(128)}) all-reduce(f32[]{:T(128)} %get-tuple-element.130, f32[]{:T(128)} %get-tuple-element.131), channel_id=1, replica_groups=mesh['row'=4,'col'=8] {'row'}, use_global_device_ids=true, to_apply=%region_4.5 | all-reduce | flops 2 | bytes 16 | tf_op jit(solution)/shard_map/psum | solution.py:96
  223.7 4.7 %collective-permute-start.11 = (f32[514,1]{1,0:T(8,128)S(1)}, f32[514,1]{1,0:T(8,128)S(1)}, u32[]{:S(2)}, u32[]{:S(2)}) collective-permute-start(f32[514,1]{1,0:T(8,128)S(1)} %get-tuple-element.160), channel_id=1, source_target_pairs={{0,1},{1,2},{2,3},{3,4},{4,5},{5,6},{6,7},{8,9},{9,10},{10,11},{11... | collective-permute-start | bytes 6176 | tf_op jit(solution)/shard_map/ppermute | solution.py:17
  228.4 4.1 %collective-permute-done.10 = f32[514,1]{1,0:T(8,128)S(1)} collective-permute-done((f32[514,1]{1,0:T(8,128)S(1)}, f32[514,1]{1,0:T(8,128)S(1)}, u32[]{:S(2)}, u32[]{:S(2)}) %collective-permute-start.10) | collective-permute-done | bytes 2088 | tf_op jit(solution)/shard_map/ppermute | solution.py:20
  232.5 4.6 %collective-permute-done.11 = f32[514,1]{1,0:T(8,128)S(1)} collective-permute-done((f32[514,1]{1,0:T(8,128)S(1)}, f32[514,1]{1,0:T(8,128)S(1)}, u32[]{:S(2)}, u32[]{:S(2)}) %collective-permute-start.11) | collective-permute-done | bytes 2088 | tf_op jit(solution)/shard_map/ppermute | solution.py:17
  237.9 2.2 collective-permute-start.13
  244.5 5.1 %collective-permute-start.15 = (f32[514,1]{1,0:T(8,128)S(1)}, f32[514,1]{1,0:T(8,128)S(1)}, u32[]{:S(2)}, u32[]{:S(2)}) collective-permute-start(f32[514,1]{1,0:T(8,128)S(1)} %get-tuple-element.158), channel_id=1, source_target_pairs={{0,1},{1,2},{2,3},{3,4},{4,5},{5,6},{6,7},{8,9},{9,10},{10,11},{11... | collective-permute-start | bytes 6176 | tf_op jit(solution)/shard_map/ppermute | solution.py:17
  249.6 3.9 %collective-permute-done.14 = f32[514,1]{1,0:T(8,128)S(1)} collective-permute-done((f32[514,1]{1,0:T(8,128)S(1)}, f32[514,1]{1,0:T(8,128)S(1)}, u32[]{:S(2)}, u32[]{:S(2)}) %collective-permute-start.14) | collective-permute-done | bytes 2088 | tf_op jit(solution)/shard_map/ppermute | solution.py:20
  253.5 7.2 %collective-permute-done.15 = f32[514,1]{1,0:T(8,128)S(1)} collective-permute-done((f32[514,1]{1,0:T(8,128)S(1)}, f32[514,1]{1,0:T(8,128)S(1)}, u32[]{:S(2)}, u32[]{:S(2)}) %collective-permute-start.15) | collective-permute-done | bytes 2088 | tf_op jit(solution)/shard_map/ppermute | solution.py:17
  260.8 2.6 multiply_reduce_fusion.2
  263.4 20.2 %all-reduce.1 = (f32[]{:T(128)}, f32[]{:T(128)}) all-reduce(f32[]{:T(128)} %get-tuple-element.113, f32[]{:T(128)} %get-tuple-element.112), channel_id=1, replica_groups=mesh['row'=4,'col'=8] {'col'}, use_global_device_ids=true, to_apply=%region_9.10 | all-reduce | flops 2 | bytes 16 | tf_op jit(solution)/shard_map/psum | solution.py:97
  283.6 6.4 %all-reduce.4 = (f32[]{:T(128)}, f32[]{:T(128)}) all-reduce(f32[]{:T(128)} %get-tuple-element.128, f32[]{:T(128)} %get-tuple-element.129), channel_id=1, replica_groups=mesh['row'=4,'col'=8] {'row'}, use_global_device_ids=true, to_apply=%region_10.11 | all-reduce | flops 2 | bytes 16 | tf_op jit(solution)/shard_map/psum | solution.py:96
  302.7 4.7 %collective-permute-start.19 = (f32[514,1]{1,0:T(8,128)S(1)}, f32[514,1]{1,0:T(8,128)S(1)}, u32[]{:S(2)}, u32[]{:S(2)}) collective-permute-start(f32[514,1]{1,0:T(8,128)S(1)} %get-tuple-element.156), channel_id=1, source_target_pairs={{0,1},{1,2},{2,3},{3,4},{4,5},{5,6},{6,7},{8,9},{9,10},{10,11},{11... | collective-permute-start | bytes 6176 | tf_op jit(solution)/shard_map/ppermute | solution.py:17
  307.4 4.1 %collective-permute-done.18 = f32[514,1]{1,0:T(8,128)S(1)} collective-permute-done((f32[514,1]{1,0:T(8,128)S(1)}, f32[514,1]{1,0:T(8,128)S(1)}, u32[]{:S(2)}, u32[]{:S(2)}) %collective-permute-start.18) | collective-permute-done | bytes 2088 | tf_op jit(solution)/shard_map/ppermute | solution.py:20
  311.5 4.6 %collective-permute-done.19 = f32[514,1]{1,0:T(8,128)S(1)} collective-permute-done((f32[514,1]{1,0:T(8,128)S(1)}, f32[514,1]{1,0:T(8,128)S(1)}, u32[]{:S(2)}, u32[]{:S(2)}) %collective-permute-start.19) | collective-permute-done | bytes 2088 | tf_op jit(solution)/shard_map/ppermute | solution.py:17
  316.9 2.2 collective-permute-start.21
  323.6 4.9 %collective-permute-start.23 = (f32[514,1]{1,0:T(8,128)S(1)}, f32[514,1]{1,0:T(8,128)S(1)}, u32[]{:S(2)}, u32[]{:S(2)}) collective-permute-start(f32[514,1]{1,0:T(8,128)S(1)} %get-tuple-element.154), channel_id=1, source_target_pairs={{0,1},{1,2},{2,3},{3,4},{4,5},{5,6},{6,7},{8,9},{9,10},{10,11},{11... | collective-permute-start | bytes 6176 | tf_op jit(solution)/shard_map/ppermute | solution.py:17
  328.5 4.1 %collective-permute-done.22 = f32[514,1]{1,0:T(8,128)S(1)} collective-permute-done((f32[514,1]{1,0:T(8,128)S(1)}, f32[514,1]{1,0:T(8,128)S(1)}, u32[]{:S(2)}, u32[]{:S(2)}) %collective-permute-start.22) | collective-permute-done | bytes 2088 | tf_op jit(solution)/shard_map/ppermute | solution.py:20
  332.6 7.2 %collective-permute-done.23 = f32[514,1]{1,0:T(8,128)S(1)} collective-permute-done((f32[514,1]{1,0:T(8,128)S(1)}, f32[514,1]{1,0:T(8,128)S(1)}, u32[]{:S(2)}, u32[]{:S(2)}) %collective-permute-start.23) | collective-permute-done | bytes 2088 | tf_op jit(solution)/shard_map/ppermute | solution.py:17
  339.8 2.5 multiply_reduce_fusion
  342.4 20.3 %all-reduce = (f32[]{:T(128)}, f32[]{:T(128)}) all-reduce(f32[]{:T(128)} %get-tuple-element.111, f32[]{:T(128)} %get-tuple-element.110), channel_id=1, replica_groups=mesh['row'=4,'col'=8] {'col'}, use_global_device_ids=true, to_apply=%region_15.16 | all-reduce | flops 2 | bytes 16 | tf_op jit(solution)/shard_map/psum | solution.py:97
  362.6 6.4 %all-reduce.3 = (f32[]{:T(128)}, f32[]{:T(128)}) all-reduce(f32[]{:T(128)} %get-tuple-element.126, f32[]{:T(128)} %get-tuple-element.127), channel_id=1, replica_groups=mesh['row'=4,'col'=8] {'row'}, use_global_device_ids=true, to_apply=%region_16.17 | all-reduce | flops 2 | bytes 16 | tf_op jit(solution)/shard_map/psum | solution.py:96
  372.8 4.3 %multiply_subtract_fusion = (f32[512,512]{1,0:T(8,128)}, f32[512,512]{1,0:T(8,128)}) fusion(f32[512,512]{1,0:T(8,128)S(1)} %multiply_subtract_fusion.1, f32[512,512]{1,0:T(8,128)} %get-tuple-element.138, f32[]{:T(128)S(6)} %div.37, f32[]{:T(128)S(6)} %div.39, f32[512,512]{1,0:T(8,128)} %get-tuple-element.139, f32[512,512]{1,0:T(8,128)} %get-tuple-element.141, ...), kind=kLoop, calls=%fused_computation.118 | loop fusion | flops 3932160 | bytes 8388628 | tf_op jit(solution)/shard_map/sub | solution.py:106
  (178 shorter events, 119.1 us)
Async XLA Ops:
  2.0 14.4 %all-to-all-start.1 = ((s32[1,16,32]{1,0,2:T(1,128)}), s32[1,16,32]{1,0,2:T(1,128)S(1)}, u32[]{:S(2)}, u32[]{:S(2)}) async-start(s32[1,16,32]{1,0,2:T(1,128)} %copy.16), calls=%async_computation.1 | async-start | bytes 32768 | tf_op jit(solution)/shard_map/all_to_all | solution.py:58
  16.4 10.4 %all-to-all-start.3 = ((bf16[1,16,32,128]{3,1,0,2:T(8,128)(2,1)}), bf16[1,16,32,128]{3,1,0,2:T(8,128)(2,1)S(1)}, u32[]{:S(2)}, u32[]{:S(2)}) async-start(bf16[1,16,32,128]{3,1,0,2:T(8,128)(2,1)} %copy.20), calls=%async_computation.3 | async-start | bytes 262144 | tf_op jit(solution)/shard_map/all_to_all | solution.py:61
  26.8 10.4 %all-to-all-start.2 = ((bf16[1,16,32,128]{3,1,0,2:T(8,128)(2,1)}), bf16[1,16,32,128]{3,1,0,2:T(8,128)(2,1)S(1)}, u32[]{:S(2)}, u32[]{:S(2)}) async-start(bf16[1,16,32,128]{3,1,0,2:T(8,128)(2,1)} %copy.18), calls=%async_computation.2 | async-start | bytes 262144 | tf_op jit(solution)/shard_map/all_to_all | solution.py:62
  37.2 13.0 %all-to-all-start = ((s32[1,16,32,128]{3,1,0,2:T(8,128)}), s32[1,16,32,128]{3,1,0,2:T(8,128)S(1)}, u32[]{:S(2)}, u32[]{:S(2)}) async-start(s32[1,16,32,128]{3,1,0,2:T(8,128)} %copy.14), calls=%async_computation | async-start | bytes 524288 | tf_op jit(solution)/shard_map/all_to_all | solution.py:57
  133.6 1.3 copy-start.5
  139.8 45.7 %copy-start.2 = (f32[1,4,128,4,128]{4,3,2,1,0:T(4,128)}, f32[1,4,128,4,128]{4,3,2,1,0:T(4,128)S(1)}, u32[]{:S(2)}) copy-start(f32[1,4,128,4,128]{4,3,2,1,0:T(4,128)S(1)} %get-tuple-element.151) | copy-start | bytes 3145732
  139.8 76.2 %copy-start.1 = (f32[1,4,128,4,128]{4,3,2,1,0:T(4,128)}, f32[1,4,128,4,128]{4,3,2,1,0:T(4,128)S(1)}, u32[]{:S(2)}) copy-start(f32[1,4,128,4,128]{4,3,2,1,0:T(4,128)S(1)} %get-tuple-element.152) | copy-start | bytes 3145732
  139.8 22.0 %copy-start = (f32[512,512]{1,0:T(8,128)S(1)}, f32[512,512]{1,0:T(8,128)}, u32[]{:S(2)}) copy-start(f32[512,512]{1,0:T(8,128)} %param.11) | copy-start | bytes 3145732
  139.9 3.4 collective-permute-start.1
  142.0 3.3 collective-permute-start
  145.4 9.8 %collective-permute-start.2 = (f32[514,1]{1,0:T(8,128)S(1)}, f32[514,1]{1,0:T(8,128)S(1)}, u32[]{:S(2)}, u32[]{:S(2)}) collective-permute-start(f32[514,1]{1,0:T(8,128)S(1)} %get-tuple-element.163), channel_id=1, source_target_pairs={{1,0},{2,1},{3,2},{4,3},{5,4},{6,5},{7,6},{9,8},{10,9},{11,10},{12... | collective-permute-start | bytes 6176 | tf_op jit(solution)/shard_map/ppermute | solution.py:20
  146.7 15.1 %collective-permute-start.3 = (f32[514,1]{1,0:T(8,128)S(1)}, f32[514,1]{1,0:T(8,128)S(1)}, u32[]{:S(2)}, u32[]{:S(2)}) collective-permute-start(f32[514,1]{1,0:T(8,128)S(1)} %get-tuple-element.164), channel_id=1, source_target_pairs={{0,1},{1,2},{2,3},{3,4},{4,5},{5,6},{6,7},{8,9},{9,10},{10,11},{11... | collective-permute-start | bytes 6176 | tf_op jit(solution)/shard_map/ppermute | solution.py:17
  162.5 3.5 collective-permute-start.5
  164.8 3.1 collective-permute-start.4
  168.0 10.3 %collective-permute-start.6 = (f32[514,1]{1,0:T(8,128)S(1)}, f32[514,1]{1,0:T(8,128)S(1)}, u32[]{:S(2)}, u32[]{:S(2)}) collective-permute-start(f32[514,1]{1,0:T(8,128)S(1)} %get-tuple-element.161), channel_id=1, source_target_pairs={{1,0},{2,1},{3,2},{4,3},{5,4},{6,5},{7,6},{9,8},{10,9},{11,10},{12... | collective-permute-start | bytes 6176 | tf_op jit(solution)/shard_map/ppermute | solution.py:20
  169.3 16.2 %collective-permute-start.7 = (f32[514,1]{1,0:T(8,128)S(1)}, f32[514,1]{1,0:T(8,128)S(1)}, u32[]{:S(2)}, u32[]{:S(2)}) collective-permute-start(f32[514,1]{1,0:T(8,128)S(1)} %get-tuple-element.162), channel_id=1, source_target_pairs={{0,1},{1,2},{2,3},{3,4},{4,5},{5,6},{6,7},{8,9},{9,10},{10,11},{11... | collective-permute-start | bytes 6176 | tf_op jit(solution)/shard_map/ppermute | solution.py:17
  217.5 3.0 collective-permute-start.9
  219.1 3.1 collective-permute-start.8
  222.3 10.1 %collective-permute-start.10 = (f32[514,1]{1,0:T(8,128)S(1)}, f32[514,1]{1,0:T(8,128)S(1)}, u32[]{:S(2)}, u32[]{:S(2)}) collective-permute-start(f32[514,1]{1,0:T(8,128)S(1)} %get-tuple-element.159), channel_id=1, source_target_pairs={{1,0},{2,1},{3,2},{4,3},{5,4},{6,5},{7,6},{9,8},{10,9},{11,10},{12... | collective-permute-start | bytes 6176 | tf_op jit(solution)/shard_map/ppermute | solution.py:20
  223.7 37.1 %copy-start.3 = (f32[1,4,128,4,128]{4,3,2,1,0:T(4,128)S(1)}, f32[1,4,128,4,128]{4,3,2,1,0:T(4,128)}, u32[]{:S(2)}) copy-start(f32[1,4,128,4,128]{4,3,2,1,0:T(4,128)} %copy-done.2) | copy-start | bytes 3145732
  223.7 13.4 %collective-permute-start.11 = (f32[514,1]{1,0:T(8,128)S(1)}, f32[514,1]{1,0:T(8,128)S(1)}, u32[]{:S(2)}, u32[]{:S(2)}) collective-permute-start(f32[514,1]{1,0:T(8,128)S(1)} %get-tuple-element.160), channel_id=1, source_target_pairs={{0,1},{1,2},{2,3},{3,4},{4,5},{5,6},{6,7},{8,9},{9,10},{10,11},{11... | collective-permute-start | bytes 6176 | tf_op jit(solution)/shard_map/ppermute | solution.py:17
  237.9 3.5 collective-permute-start.13
  240.0 3.1 collective-permute-start.12
  243.2 10.3 %collective-permute-start.14 = (f32[514,1]{1,0:T(8,128)S(1)}, f32[514,1]{1,0:T(8,128)S(1)}, u32[]{:S(2)}, u32[]{:S(2)}) collective-permute-start(f32[514,1]{1,0:T(8,128)S(1)} %get-tuple-element.157), channel_id=1, source_target_pairs={{1,0},{2,1},{3,2},{4,3},{5,4},{6,5},{7,6},{9,8},{10,9},{11,10},{12... | collective-permute-start | bytes 6176 | tf_op jit(solution)/shard_map/ppermute | solution.py:20
  244.5 16.2 %collective-permute-start.15 = (f32[514,1]{1,0:T(8,128)S(1)}, f32[514,1]{1,0:T(8,128)S(1)}, u32[]{:S(2)}, u32[]{:S(2)}) collective-permute-start(f32[514,1]{1,0:T(8,128)S(1)} %get-tuple-element.158), channel_id=1, source_target_pairs={{0,1},{1,2},{2,3},{3,4},{4,5},{5,6},{6,7},{8,9},{9,10},{10,11},{11... | collective-permute-start | bytes 6176 | tf_op jit(solution)/shard_map/ppermute | solution.py:17
  296.5 3.0 collective-permute-start.17
  298.2 3.1 collective-permute-start.16
  301.4 10.1 %collective-permute-start.18 = (f32[514,1]{1,0:T(8,128)S(1)}, f32[514,1]{1,0:T(8,128)S(1)}, u32[]{:S(2)}, u32[]{:S(2)}) collective-permute-start(f32[514,1]{1,0:T(8,128)S(1)} %get-tuple-element.155), channel_id=1, source_target_pairs={{1,0},{2,1},{3,2},{4,3},{5,4},{6,5},{7,6},{9,8},{10,9},{11,10},{12... | collective-permute-start | bytes 6176 | tf_op jit(solution)/shard_map/ppermute | solution.py:20
  302.7 37.1 %copy-start.4 = (f32[1,4,128,4,128]{4,3,2,1,0:T(4,128)S(1)}, f32[1,4,128,4,128]{4,3,2,1,0:T(4,128)}, u32[]{:S(2)}) copy-start(f32[1,4,128,4,128]{4,3,2,1,0:T(4,128)} %copy-done.2) | copy-start | bytes 3145732
  302.7 13.4 %collective-permute-start.19 = (f32[514,1]{1,0:T(8,128)S(1)}, f32[514,1]{1,0:T(8,128)S(1)}, u32[]{:S(2)}, u32[]{:S(2)}) collective-permute-start(f32[514,1]{1,0:T(8,128)S(1)} %get-tuple-element.156), channel_id=1, source_target_pairs={{0,1},{1,2},{2,3},{3,4},{4,5},{5,6},{6,7},{8,9},{9,10},{10,11},{11... | collective-permute-start | bytes 6176 | tf_op jit(solution)/shard_map/ppermute | solution.py:17
  316.9 3.5 collective-permute-start.21
  319.1 3.1 collective-permute-start.20
  322.3 10.3 %collective-permute-start.22 = (f32[514,1]{1,0:T(8,128)S(1)}, f32[514,1]{1,0:T(8,128)S(1)}, u32[]{:S(2)}, u32[]{:S(2)}) collective-permute-start(f32[514,1]{1,0:T(8,128)S(1)} %get-tuple-element.153), channel_id=1, source_target_pairs={{1,0},{2,1},{3,2},{4,3},{5,4},{6,5},{7,6},{9,8},{10,9},{11,10},{12... | collective-permute-start | bytes 6176 | tf_op jit(solution)/shard_map/ppermute | solution.py:20
  323.6 16.2 %collective-permute-start.23 = (f32[514,1]{1,0:T(8,128)S(1)}, f32[514,1]{1,0:T(8,128)S(1)}, u32[]{:S(2)}, u32[]{:S(2)}) collective-permute-start(f32[514,1]{1,0:T(8,128)S(1)} %get-tuple-element.154), channel_id=1, source_target_pairs={{0,1},{1,2},{2,3},{3,4},{4,5},{5,6},{6,7},{8,9},{9,10},{10,11},{11... | collective-permute-start | bytes 6176 | tf_op jit(solution)/shard_map/ppermute | solution.py:17
